TPU v7x, 32 devices: a whole 2x2x4 slice. The times are simulated.
32 devices in a mesh: parts: 2 (over x), seq: 16 (over z, y, core).
Axes of the slice: x: 2, y: 2, z: 4, core: 2. Of those that a mesh axis runs over, the one named last changes fastest.
Arguments:
- token_ids: int32 [4, 4], P(None, 'parts'), parts along dimension 1, may hold values from 0 to 76031
- lengths: int32 [4], P('parts'), parts along dimension 0, may hold values from 24576 to 32768, as said below
- embed_table: bfloat16 [76032, 5120], P('seq'), may hold values from -6 to 6
- attn_gain: bfloat16 [5120], replicated, may hold values from 0.25 to 1.75
- w_qkv: bfloat16 [5120, 7168], P('seq'), may hold values from -0.125 to 0.125
- qkv_bias: float32 [7168], replicated, may hold values from -8 to 8
- cache_keys: bfloat16 [4, 32768, 1024], P('parts', 'seq'), parts along dimension 0, may hold values from -300 to 300
- cache_values: bfloat16 [4, 32768, 1024], P('parts', 'seq'), parts along dimension 0, may hold values from -6 to 6
- w_out: bfloat16 [5120, 5120], P(None, 'seq'), may hold values from -0.078125 to 0.078125
- mlp_gain: bfloat16 [5120], replicated, may hold values from 0.25 to 1.75
- w_gate: bfloat16 [5120, 16384], P(None, 'seq'), may hold values from -0.078125 to 0.078125
- w_up: bfloat16 [5120, 16384], P(None, 'seq'), may hold values from -0.078125 to 0.078125
- w_down: bfloat16 [16384, 5120], P('seq'), may hold values from -0.0625 to 0.0625
Outputs:
- attended: bfloat16 [4, 4, 5120], P(None, 'parts'), parts along dimension 1
- layer_out: bfloat16 [4, 4, 5120], P(None, 'parts', 'seq'), parts along dimension 1
There are 2 independent parts, one for each index of `parts`. A program takes and returns all parts, laid end to end along the dimension named above; an argument that names none is the same for every part. Nothing has to cross between parts.
Inputs may be any that keep to these rules, and one draw needn't show every extreme that they name: Cache positions lengths[b] and later are unused; the first prompt fills the whole cache of 32768 positions.
All inputs are finite; a program needn't handle non-finite values.
Results may differ from a plain program's by a relative error of at most 0.017.
The roundings to bfloat16 on the way count: a program that leaves them out, or rounds other values in their place, can miss the bound.
Values may be sent and summed in bfloat16 or wider, within the bound.
A program may use at most 192 MiB of HBM per device.

v0:
```python
import math
import jax
import jax.numpy as jnp
from jax import lax
from jax.sharding import PartitionSpec as P

HEADS = 40
KV_HEADS = 8
HEAD_DIM = 128
NORM_EPS = 1e-06
ROPE_BASE = 1000000.0
MASKED = -1e30


def joined_2(part, axis, combine):
    gathered = jax.tree.map(lambda a: lax.all_gather(a, axis), part)

    def take(source):
        return jax.tree.map(lambda a: lax.dynamic_index_in_dim(a, source, 0, False), gathered)

    return lax.fori_loop(
        1, lax.axis_size(axis), lambda source, state: combine(state, take(source)), take(0)
    )


def rms_normalize(rows, gain):
    mean_square = jnp.mean(rows * rows, axis=-1, keepdims=True)
    return (rows * lax.rsqrt(mean_square + NORM_EPS) * gain.astype(jnp.float32)).astype(
        jnp.bfloat16
    )


def rotate(vectors, positions):
    half_dim = vectors.shape[-1] // 2
    frequency = ROPE_BASE ** (-2.0 * jnp.arange(half_dim, dtype=jnp.float32) / vectors.shape[-1])
    angles = positions.astype(jnp.float32)[..., None, None] * frequency
    cosine = jnp.cos(angles)
    sine_part = jnp.sin(angles)
    widened = vectors.astype(jnp.float32)
    first_half = widened[..., :half_dim]
    second = widened[..., half_dim:]
    joined = jnp.concatenate(
        [first_half * cosine - second * sine_part, second * cosine + first_half * sine_part],
        axis=-1,
    )
    return joined.astype(jnp.bfloat16)


def combine_partials(earlier, latter):
    top_one, total_one, sum_one = earlier
    top_two, total_two, sum_two = latter
    joined_top = jnp.maximum(top_one, top_two)
    scale_one = jnp.exp(top_one - joined_top)
    scale_two = jnp.exp(top_two - joined_top)
    return (
        joined_top,
        total_one * scale_one + total_two * scale_two,
        sum_one * scale_one[..., None] + sum_two * scale_two[..., None],
    )


def body(
    token_ids,
    lengths,
    embed_table,
    attn_gain,
    w_qkv,
    qkv_bias,
    cache_keys,
    cache_values,
    w_out,
    mlp_gain,
    w_gate,
    w_up,
    w_down,
):
    rank = lax.axis_index("seq")
    step_count, batch_count = token_ids.shape
    model_width = embed_table.shape[1]
    vocab_rows = embed_table.shape[0]
    query_width = HEADS * HEAD_DIM
    key_width = KV_HEADS * HEAD_DIM
    group_size = HEADS // KV_HEADS
    local_ids = token_ids - rank * vocab_rows
    inside = (local_ids >= 0) & (local_ids < vocab_rows)
    picked = jnp.take(embed_table, jnp.clip(local_ids, 0, vocab_rows - 1), axis=0)
    partial_rows = jnp.where(inside[..., None], picked.astype(jnp.float32), 0.0)
    stream = lax.psum(partial_rows, "seq")
    normed = rms_normalize(stream, attn_gain).reshape(-1, model_width)
    feature_rows = w_qkv.shape[0]
    normed_local = lax.dynamic_slice_in_dim(normed, rank * feature_rows, feature_rows, 1)
    joint_partial = jnp.dot(normed_local, w_qkv, preferred_element_type=jnp.float32)
    joint_summed = lax.psum(joint_partial, "seq")
    joint = (joint_summed + qkv_bias).astype(jnp.bfloat16).reshape(step_count, batch_count, -1)
    query_part = joint[..., :query_width].reshape(step_count, batch_count, HEADS, HEAD_DIM)
    key_part = joint[..., query_width : query_width + key_width].reshape(
        step_count, batch_count, KV_HEADS, HEAD_DIM
    )
    value_part = joint[..., query_width + key_width :].reshape(
        step_count, batch_count, KV_HEADS, HEAD_DIM
    )
    positions = lengths[None, :] + jnp.arange(step_count, dtype=jnp.int32)[:, None]
    queries = rotate(query_part, positions)
    new_keys = rotate(key_part, positions)
    grouped = queries.reshape(step_count, batch_count, KV_HEADS, group_size, HEAD_DIM)
    score_scale = 1.0 / math.sqrt(HEAD_DIM)
    local_len = cache_keys.shape[1]
    key_blocks = cache_keys.reshape(batch_count, local_len, KV_HEADS, HEAD_DIM)
    value_blocks = cache_values.reshape(batch_count, local_len, KV_HEADS, HEAD_DIM)
    scores = (
        jnp.einsum("sbkgd,bpkd->bkgsp", grouped, key_blocks, preferred_element_type=jnp.float32)
        * score_scale
    )
    places = rank * local_len + jnp.arange(local_len, dtype=jnp.int32)
    valid = (places[None, :] < lengths[:, None])[:, None, None, None, :]
    masked = jnp.where(valid, scores, MASKED)
    local_top = jnp.max(masked, axis=-1)
    weights = jnp.where(valid, jnp.exp(masked - local_top[..., None]), 0.0)
    local_total = jnp.sum(weights, axis=-1)
    local_sum = jnp.einsum(
        "bkgsp,bpkd->bkgsd",
        weights.astype(jnp.bfloat16),
        value_blocks,
        preferred_element_type=jnp.float32,
    )
    merged_top, merged_total, merged_sum = joined_2(
        (local_top, local_total, local_sum), "seq", combine_partials
    )
    new_scores = (
        jnp.einsum("sbkgd,tbkd->bkgst", grouped, new_keys, preferred_element_type=jnp.float32)
        * score_scale
    )
    step_index = jnp.arange(step_count, dtype=jnp.int32)
    causal = step_index[:, None] >= step_index[None, :]
    new_masked = jnp.where(causal, new_scores, MASKED)
    final_top = jnp.maximum(merged_top, jnp.max(new_masked, axis=-1))
    rescale = jnp.exp(merged_top - final_top)
    new_weights = jnp.where(causal, jnp.exp(new_masked - final_top[..., None]), 0.0)
    final_total = merged_total * rescale + jnp.sum(new_weights, axis=-1)
    final_sum = merged_sum * rescale[..., None] + jnp.einsum(
        "bkgst,tbkd->bkgsd",
        new_weights.astype(jnp.bfloat16),
        value_part,
        preferred_element_type=jnp.float32,
    )
    attended = jnp.transpose(final_sum / final_total[..., None], (3, 0, 1, 2, 4))
    attended = attended.reshape(step_count, batch_count, query_width).astype(jnp.bfloat16)
    shard_cols = w_out.shape[1]
    projected = jnp.dot(
        attended.reshape(-1, query_width), w_out, preferred_element_type=jnp.float32
    )
    stream_shard = lax.dynamic_slice_in_dim(stream, rank * shard_cols, shard_cols, 2)
    mid_shard = stream_shard + projected.reshape(step_count, batch_count, shard_cols)
    squares = lax.psum(jnp.sum(mid_shard * mid_shard, axis=-1), "seq")
    row_scale = lax.rsqrt(squares / model_width + NORM_EPS)
    gain_shard = lax.dynamic_slice_in_dim(mlp_gain, rank * shard_cols, shard_cols, 0).astype(
        jnp.float32
    )
    normed_shard = (mid_shard * row_scale[..., None] * gain_shard).astype(jnp.bfloat16)
    normed_mid = lax.all_gather(normed_shard, "seq", axis=2, tiled=True)
    flat_rows = normed_mid.reshape(-1, model_width)
    gate = jnp.dot(flat_rows, w_gate, preferred_element_type=jnp.float32)
    upper = jnp.dot(flat_rows, w_up, preferred_element_type=jnp.float32)
    hidden = (jax.nn.silu(gate) * upper).astype(jnp.bfloat16)
    down_terms = jnp.dot(hidden, w_down, preferred_element_type=jnp.float32).reshape(
        step_count, batch_count, model_width
    )
    summed = lax.psum_scatter(down_terms, "seq", scatter_dimension=2, tiled=True)
    layer_out = (mid_shard + summed).astype(jnp.bfloat16)
    return (attended, layer_out)


def solution(mesh):
    return jax.shard_map(
        body,
        mesh=mesh,
        in_specs=(
            P(None, "parts"),
            P("parts"),
            P("seq", None),
            P(),
            P("seq", None),
            P(),
            P("parts", "seq", None),
            P("parts", "seq", None),
            P(None, "seq"),
            P(),
            P(None, "seq"),
            P(None, "seq"),
            P("seq", None),
        ),
        out_specs=(P(None, "parts", None), P(None, "parts", "seq")),
        check_vma=False,
    )
```

profile of v0, /device:TPU:0, one launch (start us, length us, event | category | flops | bytes accessed | tf_op | source)
XLA Modules:
  0.0 495.7 jit_solution(8823497209833906688)
XLA Ops:
  8.3 1.9 gather_fusion
  13.4 8.8 %copy.106 = bf16[512,8,8,128]{3,2,1,0:T(8,128)(2,1)} copy(bf16[512,8,8,128]{3,1,2,0:T(8,128)(2,1)} %bitcast.100) | data formatting | bytes 16777216
  22.2 7.1 %bitcast_bitcast_fusion.1 = bf16[2,2048,8,128,1]{3,2,1,0,4:T(8,128)(2,1)} fusion(bf16[2,2048,8,128]{3,2,1,0:T(8,128)(2,1)} %bitcast.97), kind=kLoop, calls=%fused_computation.12 | loop fusion | bytes 16777216 | tf_op jit(solution)/shard_map/reshape | solution.py:108
  29.3 8.8 %copy.107 = bf16[512,8,8,128]{3,2,1,0:T(8,128)(2,1)} copy(bf16[512,8,8,128]{3,1,2,0:T(8,128)(2,1)} %bitcast.101) | data formatting | bytes 16777216
  38.1 7.0 %bitcast_bitcast_fusion = bf16[2,2048,8,128,1]{3,2,1,0,4:T(8,128)(2,1)} fusion(bf16[2,2048,8,128]{3,2,1,0:T(8,128)(2,1)} %bitcast.98), kind=kLoop, calls=%fused_computation.11 | loop fusion | bytes 16777216 | tf_op jit(solution)/shard_map/reshape | solution.py:109
  45.2 57.9 %all-reduce.3.cloned.1.call-done = f32[4,2,5120]{2,1,0:T(2,128)} async-done(((f32[4,2,5120]{2,1,0:T(2,128)}), f32[4,2,5120]{2,1,0:T(2,128)}) %all-reduce.3.cloned.1.call-update) | async-done | bytes 163856 | tf_op jit(solution)/shard_map/psum | solution.py:88
  105.3 3.7 fusion.47
  109.4 90.0 %all-reduce.5.cloned.1.call-done = f32[8,7168]{1,0:T(8,128)} async-done(((f32[8,7168]{1,0:T(8,128)}), f32[8,7168]{1,0:T(8,128)}) %all-reduce.5.cloned.1.call-update) | async-done | bytes 229392 | tf_op jit(solution)/shard_map/psum | solution.py:93
  201.2 6.3 %bitcast_reduce_fusion = (f32[2,8,5,4]{2,3,1,0:T(4,128)S(1)}, f32[2,8,4,5,2048]{4,3,2,1,0:T(8,128)S(1)}) fusion(pred[2,2048]{1,0:T(4,128)(4,1)S(1)} %broadcast_compare_fusion, bf16[2,2048,8,128,1]{3,2,1,0,4:T(8,128)(2,1)} %bitcast_bitcast_fusion.1, bf16[4,2,8,5,64]{4,3,0,2,1:T(8,128)(2,1)S(1)} %copy.69, bf16[4,2,8,5,64]{4,3,0,2,1:T(8,128)(2,1)S(1)} %copy.68), kind=kOutput, calls=%fused_computation.18 | convolution fusion | flops 169901760 | bytes 11097344 | tf_op jit(solution)/shard_map/sbkgd,bpkd->bkgsp/dot_general | solution.py:111
  207.6 3.1 fusion.4
  212.5 3.6 fusion.13
  216.2 23.1 %all-gather.1 = f32[32,8,5,4]{1,3,2,0:T(4,128)S(1)} all-gather(f32[2,8,5,4]{1,3,2,0:T(4,128)S(1)} %copy.72), channel_id=3, replica_groups=mesh['parts'=2,'seq'=16] {'seq'}, dimensions={0}, use_global_device_ids=true | all-gather | bytes 21760 | tf_op jit(solution)/shard_map/all_gather | solution.py:16
  240.1 19.3 %all-gather = f32[32,8,5,4]{1,3,2,0:T(4,128)S(1)} all-gather(f32[2,8,5,4]{1,3,2,0:T(4,128)S(1)} %copy.71), channel_id=2, replica_groups=mesh['parts'=2,'seq'=16] {'seq'}, dimensions={0}, use_global_device_ids=true | all-gather | bytes 21760 | tf_op jit(solution)/shard_map/all_gather | solution.py:16
  261.1 2.3 fusion.60
  265.1 57.2 %while.19 = (s32[]{:T(128)}, f32[2,8,5,4]{1,3,2,0:T(4,128)S(1)}, f32[2,8,5,4]{1,3,2,0:T(4,128)S(1)}, f32[2,8,5,4,128]{4,3,2,1,0:T(4,128)}, f32[16,2,8,5,4]{2,4,3...) while((s32[]{:T(128)}, f32[2,8,5,4]{1,3,2,0:T(4,128)S(1)}, ...), condition=%wide.region_6.7_spmd, body=%wide.region_5.6_spmd.sunk | while | flops 124805 | bytes 837271 | solution.py:21
  327.0 30.7 %psum.23 = f32[4,2]{1,0:T(4,128)S(1)} all-reduce(f32[4,2]{1,0:T(4,128)S(1)} %get-tuple-element.245), channel_id=1, replica_groups=mesh['parts'=2,'seq'=16] {'seq'}, use_global_device_ids=true, to_apply=%region_10.11 | all-reduce | flops 8 | bytes 64 | tf_op jit(solution)/shard_map/psum | solution.py:154
  357.9 33.2 %all_gather.27 = bf16[4,2,5120]{0,1,2:T(2,128)(2,1)} all-gather(bf16[4,2,320]{0,1,2:T(2,128)(2,1)S(1)} %copy.85), channel_id=1, replica_groups=mesh['parts'=2,'seq'=16] {'seq'}, dimensions={2}, use_global_device_ids=true | all-gather | bytes 87040 | tf_op jit(solution)/shard_map/all_gather | solution.py:160
  391.2 5.2 %copy.86 = bf16[4,2,5120]{2,1,0:T(2,128)(2,1)S(1)} copy(bf16[4,2,5120]{0,1,2:T(2,128)(2,1)} %all_gather.27) | data formatting | bytes 163840 | tf_op jit(solution)/shard_map/all_gather | solution.py:160
  396.5 5.4 %fusion.61 = f32[8,1024]{1,0:T(8,128)S(1)} fusion(bf16[8,5120]{1,0:T(8,128)(2,1)S(1)} %reshape.133, bf16[5120,1024]{1,0:T(8,128)(2,1)} %param.25), kind=kOutput, calls=%fused_computation.105 | convolution fusion | flops 83886080 | bytes 10600448 | tf_op jit(solution)/shard_map/dot_general | solution.py:162
  401.9 9.8 %fusion.30 = f32[8,5120]{1,0:T(8,128)S(1)} fusion(bf16[1024,5120]{1,0:T(8,128)(2,1)} %param.27, bf16[8,5120]{1,0:T(8,128)(2,1)S(1)} %reshape.133, bf16[5120,1024]{1,0:T(8,128)(2,1)} %param.26, f32[8,1024]{1,0:T(8,128)S(1)} %fusion.61), kind=kOutput, calls=%fused_computation.42 | convolution fusion | flops 167821312 | bytes 21250048 | tf_op jit(solution)/shard_map/dot_general | solution.py:165
  412.5 5.9 %copy.99 = f32[4,2,5120]{0,1,2:T(2,128)} copy(f32[4,2,5120]{2,1,0:T(2,128)} %reshape.134) | data formatting | bytes 327680
  418.4 6.0 %reshape.161 = f32[5120,8]{1,0:T(8,128)} reshape(f32[5120,2,4]{2,1,0:T(2,128)} %bitcast.99) | data formatting | bytes 327680
  424.4 61.2 %reduce-scatter.4.cloned.1.call-done = f32[320,8]{1,0:T(8,128)} async-done(((f32[5120,8]{1,0:T(8,128)}), f32[320,8]{1,0:T(8,128)}) %reduce-scatter.4.cloned.1.call-update) | async-done | bytes 10256
  485.5 1.9 reshape.162
  (165 shorter events, 79.1 us)
Async XLA Ops:
  7.2 317.9 %copy-start = (bf16[5120,320]{0,1:T(8,128)(2,1)S(1)}, bf16[5120,320]{0,1:T(8,128)(2,1)}, u32[]{:S(2)}) copy-start(bf16[5120,320]{0,1:T(8,128)(2,1)} %param.23) | copy-start | bytes 9830404
  7.2 95.9 %all-reduce.3.cloned.1.call-start = ((), (), s32[]{:S(2)}) async-start(), calls=%async_computation.1 | async-start | bytes 327680 | tf_op jit(solution)/shard_map/psum | solution.py:88
  11.2 188.2 %all-reduce.5.cloned.1.call-start = ((), (), s32[]{:S(2)}) async-start(), calls=%async_computation.2 | async-start | bytes 458752 | tf_op jit(solution)/shard_map/psum | solution.py:93
  45.2 154.3 %copy-start.9 = (f32[7168]{0:T(1024)S(1)}, f32[7168]{0:T(1024)}, u32[]{:S(2)}) copy-start(f32[7168]{0:T(1024)} %param.20) | copy-start | bytes 86020
  109.1 154.3 %all-gather.5.cloned.1.call-start = ((), (), s32[]{:S(2)}) async-start(), calls=%async_computation.3 | async-start | bytes 2785280 | tf_op jit(solution)/shard_map/all_gather | solution.py:16
  200.4 0.7 copy-start.5
  201.1 6.5 %slice-start = ((s8[8388608]{0:T(1024)(128)(4,1)}), s8[4194304]{0:T(1024)(128)(4,1)S(1)}, s32[]{:S(2)}) async-start(s8[8388608]{0:T(1024)(128)(4,1)} %bitcast.102), calls=%async_computation.5 | async-start | bytes 8388608
  201.2 6.4 %copy-start.4 = (bf16[4,2,8,5,64]{4,3,0,2,1:T(8,128)(2,1)}, bf16[4,2,8,5,64]{4,3,0,2,1:T(8,128)(2,1)S(1)}, u32[]{:S(2)}) copy-start(bf16[4,2,8,5,64]{4,3,0,2,1:T(8,128)(2,1)S(1)} %copy.69) | copy-start | bytes 122884
  201.2 6.4 %slice-start.1 = ((s8[8388608]{0:T(1024)(128)(4,1)}), s8[4194304]{0:T(1024)(128)(4,1)S(1)}, s32[]{:S(2)}) async-start(s8[8388608]{0:T(1024)(128)(4,1)} %bitcast.102), calls=%async_computation.6 | async-start | bytes 8388608
  207.5 3.2 copy-start.1
  211.5 274.0 %reduce-scatter.4.cloned.1.call-start = ((), (), s32[]{:S(2)}) async-start(), calls=%async_computation.4 | async-start | bytes 2785280
  239.3 0.7 copy-start.2
  259.4 0.7 copy-start.3
  325.1 32.6 %copy-start.6 = (bf16[4,2,5120]{2,1,0:T(2,128)(2,1)}, bf16[4,2,5120]{2,1,0:T(2,128)(2,1)S(1)}, u32[]{:S(2)}) copy-start(bf16[4,2,5120]{2,1,0:T(2,128)(2,1)S(1)} %convert_element_type.77) | copy-start | bytes 245764
  327.0 30.7 %copy-start.7 = (f32[4,2,320]{2,1,0:T(2,128)}, f32[4,2,320]{2,1,0:T(2,128)S(1)}, u32[]{:S(2)}) copy-start(f32[4,2,320]{2,1,0:T(2,128)S(1)} %get-tuple-element.246) | copy-start | bytes 30724
  418.4 70.1 %copy-start.8 = (f32[4,2,320]{2,1,0:T(2,128)S(1)}, f32[4,2,320]{2,1,0:T(2,128)}, u32[]{:S(2)}) copy-start(f32[4,2,320]{2,1,0:T(2,128)} %copy-done.7) | copy-start | bytes 30724
Sparse Core Ops, SparseCore 0:
  11.4 91.6 all-reduce.2
  109.2 90.1 all-reduce.4
  211.6 46.0 all-gather.4
  424.5 61.0 reduce-scatter.3
where the time goes:
time: 499 us; the launch traced here: 496 us
  waiting for transfers between devices  209 us (42%)
  blocking collectives  106 us (21%)
  local copies, waits for them, and re-layouts  78.3 us (16%)
  other arithmetic  53.3 us (11%)
  matrix products  34 us (7%)
  between operations  14.1 us (3%)
    psum x1, waiting for transfers between devices, body(): joint_summed = lax.psum(joint_partial, 'seq')  90 us
    unnamed x5, waiting for transfers between devices  61.2 us
    psum x1, waiting for transfers between devices, body(): stream = lax.psum(partial_rows, 'seq')  57.9 us
    all_gather x2, blocking collectives, joined_2(): gathered = jax.tree.map(lambda a: lax.all_gather(a, axis), part)  42.5 us
    all_gather x1, blocking collectives, body(): normed_mid = lax.all_gather(normed_shard, 'seq', axis=2, tiled=True)  33.2 us
    unnamed x29, local copies, waits for them, and re-layouts  33.1 us
    psum x1, blocking collectives, body(): squares = lax.psum(jnp.sum(mid_shard * mid_shard, axis=-1), 'seq')  30.7 us
    add x15, other arithmetic, combine_partials(): sum_one * scale_one[..., None] + sum_two * scale_two[..., None]  27.3 us
  transfers between devices with their start and end apart: 4, of which 3 were waited for; matrix products, arithmetic and copies ran while one was open for 8% of the time, Pallas kernels for 0%

commit v1 on v0

--- a/solution.py
+++ b/solution.py
@@ -157,7 +157,7 @@
         jnp.float32
     )
     normed_shard = (mid_shard * row_scale[..., None] * gain_shard).astype(jnp.bfloat16)
-    normed_mid = lax.all_gather(normed_shard, "seq", axis=2, tiled=True)
+    normed_mid = jnp.concatenate(lax.all_gather(normed_shard, "seq"), axis=2)
     flat_rows = normed_mid.reshape(-1, model_width)
     gate = jnp.dot(flat_rows, w_gate, preferred_element_type=jnp.float32)
     upper = jnp.dot(flat_rows, w_up, preferred_element_type=jnp.float32)

time: 499 us -> 479 us (0.960)
  blocking collectives: 106 us -> 90.7 us
  local copies, waits for them, and re-layouts: 78.3 us -> 73 us
    all_gather x1, blocking collectives: 33.2 us -> 17.6 us  [body(): normed_mid = jnp.concatenate(lax.all_gather(normed_shard, 'seq'), axis=2)]
    all_gather x1, local copies, waits for them, and re-layouts: 5.21 us -> 0.01 us  [body(): normed_mid = jnp.concatenate(lax.all_gather(normed_shard, 'seq'), axis=2)]
  transfers between devices with their start and end apart: 4 -> 4, of which waited for: 3 -> 3; matrix products, arithmetic and copies ran while one was open for 8% -> 9% of each run, Pallas kernels for 0% -> 0%
where the time goes in v1:
time: 479 us; the launch traced here: 476 us
  waiting for transfers between devices  211 us (44%)
  blocking collectives  90.7 us (19%)
  local copies, waits for them, and re-layouts  73 us (15%)
  other arithmetic  53.3 us (11%)
  matrix products  34 us (7%)
  between operations  14.1 us (3%)
    psum x1, waiting for transfers between devices, body(): joint_summed = lax.psum(joint_partial, 'seq')  90 us
    unnamed x5, waiting for transfers between devices  62.6 us
    psum x1, waiting for transfers between devices, body(): stream = lax.psum(partial_rows, 'seq')  57.9 us
    all_gather x2, blocking collectives, joined_2(): gathered = jax.tree.map(lambda a: lax.all_gather(a, axis), part)  42.5 us
    unnamed x29, local copies, waits for them, and re-layouts  33.1 us
    psum x1, blocking collectives, body(): squares = lax.psum(jnp.sum(mid_shard * mid_shard, axis=-1), 'seq')  30.7 us
    add x15, other arithmetic, combine_partials(): sum_one * scale_one[..., None] + sum_two * scale_two[..., None]  27.3 us
    all_gather x1, blocking collectives, body(): normed_mid = jnp.concatenate(lax.all_gather(normed_shard, 'seq'), axis=2)  17.6 us
  transfers between devices with their start and end apart: 4, of which 3 were waited for; matrix products, arithmetic and copies ran while one was open for 9% of the time, Pallas kernels for 0%

profile of v1, /device:TPU:0, one launch (start us, length us, event | category | flops | bytes accessed | tf_op | source)
XLA Modules:
  0.0 476.1 jit_solution(7484312634553994906)
XLA Ops:
  8.3 1.9 gather_fusion
  13.4 8.8 %copy.105 = bf16[512,8,8,128]{3,2,1,0:T(8,128)(2,1)} copy(bf16[512,8,8,128]{3,1,2,0:T(8,128)(2,1)} %bitcast.106) | data formatting | bytes 16777216
  22.2 7.1 %bitcast_bitcast_fusion.1 = bf16[2,2048,8,128,1]{3,2,1,0,4:T(8,128)(2,1)} fusion(bf16[2,2048,8,128]{3,2,1,0:T(8,128)(2,1)} %bitcast.103), kind=kLoop, calls=%fused_computation.12 | loop fusion | bytes 16777216 | tf_op jit(solution)/shard_map/reshape | solution.py:108
  29.3 8.8 %copy.106 = bf16[512,8,8,128]{3,2,1,0:T(8,128)(2,1)} copy(bf16[512,8,8,128]{3,1,2,0:T(8,128)(2,1)} %bitcast.107) | data formatting | bytes 16777216
  38.1 7.0 %bitcast_bitcast_fusion = bf16[2,2048,8,128,1]{3,2,1,0,4:T(8,128)(2,1)} fusion(bf16[2,2048,8,128]{3,2,1,0:T(8,128)(2,1)} %bitcast.104), kind=kLoop, calls=%fused_computation.11 | loop fusion | bytes 16777216 | tf_op jit(solution)/shard_map/reshape | solution.py:109
  45.2 57.9 %all-reduce.3.cloned.1.call-done = f32[4,2,5120]{2,1,0:T(2,128)} async-done(((f32[4,2,5120]{2,1,0:T(2,128)}), f32[4,2,5120]{2,1,0:T(2,128)}) %all-reduce.3.cloned.1.call-update) | async-done | bytes 163856 | tf_op jit(solution)/shard_map/psum | solution.py:88
  105.3 3.7 fusion.47
  109.4 90.0 %all-reduce.5.cloned.1.call-done = f32[8,7168]{1,0:T(8,128)} async-done(((f32[8,7168]{1,0:T(8,128)}), f32[8,7168]{1,0:T(8,128)}) %all-reduce.5.cloned.1.call-update) | async-done | bytes 229392 | tf_op jit(solution)/shard_map/psum | solution.py:93
  201.2 6.3 %bitcast_reduce_fusion = (f32[2,8,5,4]{2,3,1,0:T(4,128)S(1)}, f32[2,8,4,5,2048]{4,3,2,1,0:T(8,128)S(1)}) fusion(pred[2,2048]{1,0:T(4,128)(4,1)S(1)} %broadcast_compare_fusion, bf16[2,2048,8,128,1]{3,2,1,0,4:T(8,128)(2,1)} %bitcast_bitcast_fusion.1, bf16[4,2,8,5,64]{4,3,0,2,1:T(8,128)(2,1)S(1)} %copy.69, bf16[4,2,8,5,64]{4,3,0,2,1:T(8,128)(2,1)S(1)} %copy.68), kind=kOutput, calls=%fused_computation.18 | convolution fusion | flops 169901760 | bytes 11097344 | tf_op jit(solution)/shard_map/sbkgd,bpkd->bkgsp/dot_general | solution.py:111
  207.6 3.1 fusion.4
  212.5 3.6 fusion.13
  216.2 23.1 %all-gather.1 = f32[32,8,5,4]{1,3,2,0:T(4,128)S(1)} all-gather(f32[2,8,5,4]{1,3,2,0:T(4,128)S(1)} %copy.72), channel_id=3, replica_groups=mesh['parts'=2,'seq'=16] {'seq'}, dimensions={0}, use_global_device_ids=true | all-gather | bytes 21760 | tf_op jit(solution)/shard_map/all_gather | solution.py:16
  240.1 19.3 %all-gather = f32[32,8,5,4]{1,3,2,0:T(4,128)S(1)} all-gather(f32[2,8,5,4]{1,3,2,0:T(4,128)S(1)} %copy.71), channel_id=2, replica_groups=mesh['parts'=2,'seq'=16] {'seq'}, dimensions={0}, use_global_device_ids=true | all-gather | bytes 21760 | tf_op jit(solution)/shard_map/all_gather | solution.py:16
  261.1 2.3 fusion.60
  265.1 57.2 %while.19 = (s32[]{:T(128)}, f32[2,8,5,4]{1,3,2,0:T(4,128)S(1)}, f32[2,8,5,4]{1,3,2,0:T(4,128)S(1)}, f32[2,8,5,4,128]{4,3,2,1,0:T(4,128)}, f32[16,2,8,5,4]{2,4,3...) while((s32[]{:T(128)}, f32[2,8,5,4]{1,3,2,0:T(4,128)S(1)}, ...), condition=%wide.region_6.7_spmd, body=%wide.region_5.6_spmd.sunk | while | flops 124805 | bytes 837271 | solution.py:21
  325.1 1.8 multiply_reduce_fusion.1
  327.0 30.7 %psum.23 = f32[4,2]{1,0:T(4,128)S(1)} all-reduce(f32[4,2]{1,0:T(4,128)S(1)} %get-tuple-element.245), channel_id=1, replica_groups=mesh['parts'=2,'seq'=16] {'seq'}, use_global_device_ids=true, to_apply=%region_10.11 | all-reduce | flops 8 | bytes 64 | tf_op jit(solution)/shard_map/psum | solution.py:154
  357.8 17.6 %all-gather.3 = bf16[64,2,320]{2,1,0:T(2,128)(2,1)S(1)} all-gather(bf16[4,2,320]{2,1,0:T(2,128)(2,1)S(1)} %multiply_convert_fusion.1), channel_id=5, replica_groups=mesh['parts'=2,'seq'=16] {'seq'}, dimensions={0}, use_global_device_ids=true | all-gather | bytes 87040 | tf_op jit(solution)/shard_map/all_gather | solution.py:160
  375.5 5.4 %fusion.61 = f32[8,1024]{1,0:T(8,128)S(1)} fusion(bf16[8,5120]{1,0:T(8,128)(2,1)S(1)} %reshape_reshape.3, bf16[5120,1024]{1,0:T(8,128)(2,1)} %param.25), kind=kOutput, calls=%fused_computation.106 | convolution fusion | flops 83886080 | bytes 10600448 | tf_op jit(solution)/shard_map/dot_general | solution.py:162
  380.9 9.8 %fusion.30 = f32[8,5120]{1,0:T(8,128)S(1)} fusion(bf16[1024,5120]{1,0:T(8,128)(2,1)} %param.27, bf16[8,5120]{1,0:T(8,128)(2,1)S(1)} %reshape_reshape.3, bf16[5120,1024]{1,0:T(8,128)(2,1)} %param.26, f32[8,1024]{1,0:T(8,128)S(1)} %fusion.61), kind=kOutput, calls=%fused_computation.42 | convolution fusion | flops 167821312 | bytes 21250048 | tf_op jit(solution)/shard_map/dot_general | solution.py:165
  391.5 5.9 %copy.98 = f32[4,2,5120]{0,1,2:T(2,128)} copy(f32[4,2,5120]{2,1,0:T(2,128)} %reshape.134) | data formatting | bytes 327680
  397.4 6.0 %reshape.162 = f32[5120,8]{1,0:T(8,128)} reshape(f32[5120,2,4]{2,1,0:T(2,128)} %bitcast.105) | data formatting | bytes 327680
  403.4 62.6 %reduce-scatter.4.cloned.1.call-done = f32[320,8]{1,0:T(8,128)} async-done(((f32[5120,8]{1,0:T(8,128)}), f32[320,8]{1,0:T(8,128)}) %reduce-scatter.4.cloned.1.call-update) | async-done | bytes 10256
  466.0 1.9 reshape.163
  (164 shorter events, 77.2 us)
Async XLA Ops:
  7.2 317.9 %copy-start = (bf16[5120,320]{0,1:T(8,128)(2,1)S(1)}, bf16[5120,320]{0,1:T(8,128)(2,1)}, u32[]{:S(2)}) copy-start(bf16[5120,320]{0,1:T(8,128)(2,1)} %param.23) | copy-start | bytes 9830404
  7.2 95.9 %all-reduce.3.cloned.1.call-start = ((), (), s32[]{:S(2)}) async-start(), calls=%async_computation.1 | async-start | bytes 327680 | tf_op jit(solution)/shard_map/psum | solution.py:88
  11.2 188.2 %all-reduce.5.cloned.1.call-start = ((), (), s32[]{:S(2)}) async-start(), calls=%async_computation.2 | async-start | bytes 458752 | tf_op jit(solution)/shard_map/psum | solution.py:93
  45.2 154.3 %copy-start.9 = (f32[7168]{0:T(1024)S(1)}, f32[7168]{0:T(1024)}, u32[]{:S(2)}) copy-start(f32[7168]{0:T(1024)} %param.20) | copy-start | bytes 86020
  109.1 154.3 %all-gather.6.cloned.1.call-start = ((), (), s32[]{:S(2)}) async-start(), calls=%async_computation.3 | async-start | bytes 2785280 | tf_op jit(solution)/shard_map/all_gather | solution.py:16
  200.4 0.7 copy-start.5
  201.1 6.5 %slice-start = ((s8[8388608]{0:T(1024)(128)(4,1)}), s8[4194304]{0:T(1024)(128)(4,1)S(1)}, s32[]{:S(2)}) async-start(s8[8388608]{0:T(1024)(128)(4,1)} %bitcast.108), calls=%async_computation.5 | async-start | bytes 8388608
  201.2 6.4 %copy-start.4 = (bf16[4,2,8,5,64]{4,3,0,2,1:T(8,128)(2,1)}, bf16[4,2,8,5,64]{4,3,0,2,1:T(8,128)(2,1)S(1)}, u32[]{:S(2)}) copy-start(bf16[4,2,8,5,64]{4,3,0,2,1:T(8,128)(2,1)S(1)} %copy.69) | copy-start | bytes 122884
  201.2 6.4 %slice-start.1 = ((s8[8388608]{0:T(1024)(128)(4,1)}), s8[4194304]{0:T(1024)(128)(4,1)S(1)}, s32[]{:S(2)}) async-start(s8[8388608]{0:T(1024)(128)(4,1)} %bitcast.108), calls=%async_computation.6 | async-start | bytes 8388608
  207.5 3.2 copy-start.1
  211.5 254.5 %reduce-scatter.4.cloned.1.call-start = ((), (), s32[]{:S(2)}) async-start(), calls=%async_computation.4 | async-start | bytes 2785280
  239.3 0.7 copy-start.2
  259.4 0.7 copy-start.3
  325.1 50.2 %copy-start.6 = (bf16[4,2,5120]{2,1,0:T(2,128)(2,1)}, bf16[4,2,5120]{2,1,0:T(2,128)(2,1)S(1)}, u32[]{:S(2)}) copy-start(bf16[4,2,5120]{2,1,0:T(2,128)(2,1)S(1)} %convert_element_type.77) | copy-start | bytes 245764
  327.0 48.4 %copy-start.7 = (f32[4,2,320]{2,1,0:T(2,128)}, f32[4,2,320]{2,1,0:T(2,128)S(1)}, u32[]{:S(2)}) copy-start(f32[4,2,320]{2,1,0:T(2,128)S(1)} %get-tuple-element.246) | copy-start | bytes 30724
  397.4 71.5 %copy-start.8 = (f32[4,2,320]{2,1,0:T(2,128)S(1)}, f32[4,2,320]{2,1,0:T(2,128)}, u32[]{:S(2)}) copy-start(f32[4,2,320]{2,1,0:T(2,128)} %copy-done.7) | copy-start | bytes 30724
Sparse Core Ops, SparseCore 0:
  11.4 91.6 all-reduce.2
  109.2 90.1 all-reduce.4
  211.6 46.0 all-gather.5
  403.5 62.4 reduce-scatter.3
